TPU v7x, 32 devices: a whole 2x2x4 slice. The times are simulated.
32 devices in a mesh: row: 8 (over z, core), col: 4 (over y, x).
Axes of the slice: x: 2, y: 2, z: 4, core: 2. Of those that a mesh axis runs over, the one named last changes fastest.
Arguments:
- embedding: bfloat16 [256, 128], P('col'), may hold values from -6 to 6
- dilation: int32 [2], replicated, may hold values from 1 to 4, as said below
- kernel: bfloat16 [3, 3, 48, 128], replicated, may hold values from -0.1875 to 0.1875
- kernel_bias: float32 [48], replicated, may hold values from -3 to 3
- mixing: bfloat16 [5, 48], replicated, may hold values from -0.875 to 0.875
- mixing_bias: float32 [5], replicated, may hold values from -3 to 3
- cotangent: bfloat16 [5, 256, 256], P(None, 'row', 'col'), may hold values from -0.375 to 0.375
Outputs:
- contact: float32 [5, 256, 256], P(None, 'row', 'col')
- embedding_grad: float32 [256, 128], P('col')
- kernel_grad: float32 [3, 3, 48, 128], replicated
Inputs may be any that keep to these rules, and one draw needn't show every extreme that they name: `dilation`: the larger of the two rates is exactly 4.
All inputs are finite; a program needn't handle non-finite values.
Results may differ from a plain program's by a relative error of at most 0.019.
The roundings to bfloat16 on the way count: a program that leaves them out, or rounds other values in their place, can miss the bound.
Values may be sent and summed in bfloat16 or wider, within the bound.
No kernel may reach another device: no remote copies, remote signals or barrier semaphores. Data moves between devices by JAX's collectives and lax.ppermute only.
A program may use at most 64 MiB of HBM per device.

v0:
```python
import jax
import jax.numpy as jnp
from jax import lax
from jax.sharding import PartitionSpec as P

DMAX = 4


def shifted(value, axis, by):
    peers = lax.axis_size(axis)
    pairs = [(i, i + by) for i in range(peers) if 0 <= i + by < peers]
    return lax.ppermute(value, axis, pairs)


def tap_list():
    return [(tap_row, tap_col) for tap_row in (-1, 0, 1) for tap_col in (-1, 0, 1)]


def narrow(values):
    return values.astype(jnp.bfloat16)


def add_into(target, position, update):
    current = lax.dynamic_slice_in_dim(target, position, update.shape[0], 0)
    return lax.dynamic_update_slice_in_dim(target, current + update, position, 0)


def fold_edges(extended, margin, count, before, after):
    inner_rows = extended[margin : margin + count]
    inner_rows = inner_rows + jnp.pad(before, ((0, count - margin), (0, 0)))
    return inner_rows + jnp.pad(after, ((count - margin, 0), (0, 0)))


def per_device(embedding, dilation, kernel, kernel_bias, mixing, mixing_bias, cotangent):
    highest = lax.Precision.HIGHEST
    row_rate = dilation[0]
    col_rate = dilation[1]
    margin = DMAX
    channels = embedding.shape[1]
    filters = kernel.shape[2]
    row_count = cotangent.shape[1]
    col_count = cotangent.shape[2]
    col_devices = lax.axis_size("col")
    bins_total = col_count * col_devices
    row_index = lax.axis_index("row")
    col_index = lax.axis_index("col")
    row_start = row_index * row_count
    col_start = col_index * col_count
    every_bin = lax.all_gather(embedding, "col", axis=0, tiled=True)
    padded = jnp.pad(every_bin, ((margin, margin), (0, 0)))
    row_values = lax.dynamic_slice_in_dim(padded, row_start, row_count + 2 * margin, 0)
    col_values = lax.dynamic_slice_in_dim(padded, col_start, col_count + 2 * margin, 0)
    row_places = row_start - margin + jnp.arange(row_count + 2 * margin, dtype=jnp.int32)
    col_places = col_start - margin + jnp.arange(col_count + 2 * margin, dtype=jnp.int32)
    row_inside = ((row_places >= 0) & (row_places < bins_total)).astype(jnp.float32)
    col_inside = ((col_places >= 0) & (col_places < bins_total)).astype(jnp.float32)
    pairs = narrow(
        0.5
        * (row_values.astype(jnp.float32)[:, None, :] + col_values.astype(jnp.float32)[None, :, :])
    )
    keep_mask = (row_inside[:, None] * col_inside[None, :]).astype(jnp.bfloat16)
    pairs = pairs * keep_mask[:, :, None]
    zero_index = jnp.zeros((), jnp.int32)

    def slicer(tap_row, tap_col, mirrored):
        if mirrored:
            first_at, second_at = (margin + tap_col * col_rate, margin + tap_row * row_rate)
        else:
            first_at, second_at = (margin + tap_row * row_rate, margin + tap_col * col_rate)
        return lax.dynamic_slice(
            pairs, (first_at, second_at, zero_index), (row_count, col_count, channels)
        )

    def convolve(mirrored):
        running = jnp.zeros((filters, row_count, col_count), jnp.float32)
        for tap_row, tap_col in tap_list():
            tap_piece = slicer(tap_row, tap_col, mirrored)
            running = running + jnp.einsum(
                "ijc,fc->fij",
                tap_piece,
                kernel[tap_row + 1, tap_col + 1],
                preferred_element_type=jnp.float32,
            )
        return running + kernel_bias[:, None, None]

    direct = convolve(False)
    mirror = convolve(True)
    direct_act = narrow(jax.nn.relu(direct))
    mirror_act = narrow(jax.nn.relu(mirror))

    def mix_map(activation):
        return (
            jnp.einsum("tf,fij->tij", mixing, activation, preferred_element_type=jnp.float32)
            + mixing_bias[:, None, None]
        )

    contact = 0.5 * mix_map(direct_act) + 0.5 * mix_map(mirror_act)
    guide_grad = narrow(
        0.5 * jnp.einsum("tf,tij->fij", mixing, cotangent, preferred_element_type=jnp.float32)
    )
    grad_direct = jnp.where(direct > 0, guide_grad, jnp.zeros_like(guide_grad))
    grad_mirror = jnp.where(mirror > 0, guide_grad, jnp.zeros_like(guide_grad))
    updates = []
    for tap_row, tap_col in tap_list():
        tap_term = jnp.einsum(
            "fij,ijc->fc",
            grad_direct,
            slicer(tap_row, tap_col, False),
            preferred_element_type=jnp.float32,
        )
        tap_term = tap_term + jnp.einsum(
            "fij,ijc->fc",
            grad_mirror,
            slicer(tap_row, tap_col, True),
            preferred_element_type=jnp.float32,
        )
        updates.append(tap_term)
    kernel_terms = jnp.stack(updates).reshape(3, 3, filters, channels)
    kernel_grad = lax.psum(kernel_terms, ("row", "col"))

    def col_mask(shift):
        return lax.dynamic_slice_in_dim(col_inside, margin + shift, col_count, 0).astype(
            jnp.bfloat16
        )

    def row_mask(shift):
        return lax.dynamic_slice_in_dim(row_inside, margin + shift, row_count, 0).astype(
            jnp.bfloat16
        )

    direct_rows = [
        jnp.einsum(
            "fij,j->fi",
            grad_direct,
            col_mask(tap_step * col_rate),
            preferred_element_type=jnp.float32,
        )
        for tap_step in (-1, 0, 1)
    ]
    direct_cols = [
        jnp.einsum(
            "fij,i->fj",
            grad_direct,
            row_mask(tap_step * row_rate),
            preferred_element_type=jnp.float32,
        )
        for tap_step in (-1, 0, 1)
    ]
    mirror_rows = [
        jnp.einsum(
            "fij,j->fi",
            grad_mirror,
            col_mask(tap_step * row_rate),
            preferred_element_type=jnp.float32,
        )
        for tap_step in (-1, 0, 1)
    ]
    mirror_cols = [
        jnp.einsum(
            "fij,i->fj",
            grad_mirror,
            row_mask(tap_step * col_rate),
            preferred_element_type=jnp.float32,
        )
        for tap_step in (-1, 0, 1)
    ]
    row_grad = jnp.zeros((row_count + 2 * margin, channels), jnp.float32)
    col_grad = jnp.zeros((col_count + 2 * margin, channels), jnp.float32)
    for tap_row, tap_col in tap_list():
        tap_weight = kernel[tap_row + 1, tap_col + 1].astype(jnp.float32)
        row_grad = add_into(
            row_grad,
            margin + tap_row * row_rate,
            jnp.einsum("fi,fc->ic", direct_rows[tap_col + 1], tap_weight, precision=highest),
        )
        row_grad = add_into(
            row_grad,
            margin + tap_col * col_rate,
            jnp.einsum("fi,fc->ic", mirror_rows[tap_row + 1], tap_weight, precision=highest),
        )
        col_grad = add_into(
            col_grad,
            margin + tap_col * col_rate,
            jnp.einsum("fj,fc->jc", direct_cols[tap_row + 1], tap_weight, precision=highest),
        )
        col_grad = add_into(
            col_grad,
            margin + tap_row * row_rate,
            jnp.einsum("fj,fc->jc", mirror_cols[tap_col + 1], tap_weight, precision=highest),
        )
    upper_rows = shifted(row_grad[:margin], "row", -1)
    lower_rows = shifted(row_grad[row_count + margin :], "row", 1)
    inner_rows = fold_edges(row_grad, margin, row_count, lower_rows, upper_rows)
    row_total = lax.psum(inner_rows, "col")
    every_row = lax.all_gather(row_total, "row", axis=0, tiled=True)
    row_share = lax.dynamic_slice_in_dim(every_row, col_start, col_count, 0)
    left_cols = shifted(col_grad[:margin], "col", -1)
    right_cols = shifted(col_grad[col_count + margin :], "col", 1)
    inner_cols = fold_edges(col_grad, margin, col_count, right_cols, left_cols)
    col_total = lax.psum(inner_cols, "row")
    embedding_grad = 0.5 * row_share + 0.5 * col_total
    return (contact, embedding_grad, kernel_grad)


def solution(mesh):
    return jax.shard_map(
        per_device,
        mesh=mesh,
        in_specs=(P("col", None), P(), P(), P(), P(), P(), P(None, "row", "col")),
        out_specs=(P(None, "row", "col"), P("col", None), P()),
        check_vma=False,
    )
```

profile of v0, /device:TPU:8, one launch (start us, length us, event | category | flops | bytes accessed | tf_op | source)
XLA Modules:
  0.0 207.0 jit_solution(6077568537397466937)
XLA Ops:
  7.2 1.3 fusion.300
  13.8 8.4 %all_gather.6 = bf16[256,128]{1,0:T(8,128)(2,1)S(1)} all-gather(bf16[64,128]{1,0:T(8,128)(2,1)} %param.7), channel_id=1, replica_groups=mesh['row'=8,'col'=4] {'col'}, dimensions={0}, use_global_device_ids=true | all-gather | bytes 81920 | tf_op jit(solution)/shard_map/all_gather | solution.py:49
  22.3 0.5 fusion.35
  22.8 0.6 fusion.72
  23.4 0.6 fusion.68
  24.0 0.6 convolution_add_fusion.13
  24.7 0.6 convolution_add_fusion.12
  25.3 0.6 fusion.3
  26.0 0.6 convolution_add_fusion.10
  26.6 0.6 convolution_add_fusion.9
  27.2 0.6 convolution_add_fusion.8
  27.9 0.6 fusion.59
  28.5 0.6 convolution_add_fusion.6
  29.1 0.6 convolution_add_fusion.5
  29.8 0.5 copy-done.3
  30.3 0.6 fusion.1
  30.9 0.6 convolution_add_fusion.3
  31.5 0.6 convolution_add_fusion.2
  32.2 0.6 convolution_add_fusion.1
  32.8 0.6 fusion.2
  33.4 0.6 fusion
  34.1 0.4 bitcast_select_fusion
  44.9 1.3 collective-permute-start.3
  46.2 4.7 %collective-permute-start.2 = (f32[4,128]{1,0:T(4,128)S(1)}, f32[4,128]{1,0:T(4,128)S(1)}, u32[]{:S(2)}, u32[]{:S(2)}) collective-permute-start(f32[4,128]{1,0:T(4,128)S(1)} %get-tuple-element.8), channel_id=1, source_target_pairs={{0,1},{1,2},{2,3},{4,5},{5,6},{6,7},{8,9},{9,10},{10,11},{12,13},{... | collective-permute-start | bytes 6152 | tf_op jit(solution)/shard_map/ppermute | solution.py:12
  50.9 0.5 fusion.272
  51.4 0.5 fusion.270
  51.9 0.5 fusion.264
  52.4 0.5 fusion.268
  52.9 0.5 fusion.266
  56.5 0.5 fusion.262
  59.9 1.9 collective-permute-start.1
  61.8 2.4 %collective-permute-start = (f32[4,128]{1,0:T(4,128)S(1)}, f32[4,128]{1,0:T(4,128)S(1)}, u32[]{:S(2)}, u32[]{:S(2)}) collective-permute-start(f32[4,128]{1,0:T(4,128)S(1)} %get-tuple-element.10), channel_id=1, source_target_pairs={{0,4},{4,8},{8,12},{12,16},{16,20},{20,24},{24,28},{1,5},{5,9},{9,... | collective-permute-start | bytes 6152 | tf_op jit(solution)/shard_map/ppermute | solution.py:12
  67.4 0.3 fusion.13
  67.8 0.3 fusion.16
  68.1 0.3 fusion.19
  68.4 0.3 fusion.22
  68.8 0.3 fusion.25
  69.1 0.3 fusion.28
  69.4 0.3 fusion.31
  69.8 0.3 fusion.34
  70.1 0.7 copy-done.4
  71.2 0.7 copy.11
  71.8 24.8 %psum.22 = f32[64,128]{1,0:T(8,128)S(1)} all-reduce(f32[64,128]{1,0:T(8,128)S(1)} %fusion.93), channel_id=1, replica_groups=mesh['row'=8,'col'=4] {'row'}, use_global_device_ids=true, to_apply=%region_1.2 | all-reduce | flops 8192 | bytes 65536 | tf_op jit(solution)/shard_map/psum | solution.py:200
  96.7 15.8 %psum.21 = f32[32,128]{1,0:T(8,128)S(1)} all-reduce(f32[32,128]{1,0:T(8,128)S(1)} %fusion.95), channel_id=1, replica_groups=mesh['row'=8,'col'=4] {'col'}, use_global_device_ids=true, to_apply=%region_0.1 | all-reduce | flops 4096 | bytes 32768 | tf_op jit(solution)/shard_map/psum | solution.py:194
  112.5 14.2 %all_gather.7 = f32[256,128]{1,0:T(8,128)S(1)} all-gather(f32[32,128]{1,0:T(8,128)S(1)} %psum.21), channel_id=1, replica_groups=mesh['row'=8,'col'=4] {'row'}, dimensions={0}, use_global_device_ids=true | all-gather | bytes 147456 | tf_op jit(solution)/shard_map/all_gather | solution.py:195
  126.7 0.6 add_multiply_fusion
  127.3 71.2 %all-reduce.7.cloned.1.call-done = f32[3,3,48,128]{3,2,1,0:T(8,128)} async-done(((f32[3,3,48,128]{3,2,1,0:T(8,128)}), f32[3,3,48,128]{3,2,1,0:T(8,128)}) %all-reduce.7.cloned.1.call-update) | async-done | bytes 221200 | tf_op jit(solution)/shard_map/psum | solution.py:119
  198.5 1.6 copy.87
  (123 shorter events, 19.6 us)
Async XLA Ops:
  7.2 26.9 %copy-start = (bf16[5,32,64]{2,1,0:T(8,128)(2,1)S(1)}, bf16[5,32,64]{2,1,0:T(8,128)(2,1)}, u32[]{:S(2)}) copy-start(bf16[5,32,64]{2,1,0:T(8,128)(2,1)} %param.13) | copy-start | bytes 61444
  7.2 15.6 %copy-start.1 = (bf16[3,3,48,128]{3,2,1,0:T(8,128)(2,1)S(1)}, bf16[3,3,48,128]{3,2,1,0:T(8,128)(2,1)}, u32[]{:S(2)}) copy-start(bf16[3,3,48,128]{3,2,1,0:T(8,128)(2,1)} %param.9) | copy-start | bytes 331780
  7.2 191.3 %all-reduce.7.cloned.1.call-start = ((), (), s32[]{:S(2)}) async-start(), calls=%async_computation | async-start | bytes 442368 | tf_op jit(solution)/shard_map/psum | solution.py:119
  23.4 1.9 copy-start.2
  29.1 1.1 copy-start.3
  32.2 0.7 copy-start.6
  33.4 0.7 copy-start.5
  44.9 27.0 %collective-permute-start.3 = (f32[4,128]{1,0:T(4,128)S(1)}, f32[4,128]{1,0:T(4,128)S(1)}, u32[]{:S(2)}, u32[]{:S(2)}) collective-permute-start(f32[4,128]{1,0:T(4,128)S(1)} %get-tuple-element.9), channel_id=1, source_target_pairs={{1,0},{2,1},{3,2},{5,4},{6,5},{7,6},{9,8},{10,9},{11,10},{13,12},{... | collective-permute-start | bytes 6152 | tf_op jit(solution)/shard_map/ppermute | solution.py:12
  46.2 25.7 %collective-permute-start.2 = (f32[4,128]{1,0:T(4,128)S(1)}, f32[4,128]{1,0:T(4,128)S(1)}, u32[]{:S(2)}, u32[]{:S(2)}) collective-permute-start(f32[4,128]{1,0:T(4,128)S(1)} %get-tuple-element.8), channel_id=1, source_target_pairs={{0,1},{1,2},{2,3},{4,5},{5,6},{6,7},{8,9},{9,10},{10,11},{12,13},{... | collective-permute-start | bytes 6152 | tf_op jit(solution)/shard_map/ppermute | solution.py:12
  59.9 36.8 %collective-permute-start.1 = (f32[4,128]{1,0:T(4,128)S(1)}, f32[4,128]{1,0:T(4,128)S(1)}, u32[]{:S(2)}, u32[]{:S(2)}) collective-permute-start(f32[4,128]{1,0:T(4,128)S(1)} %get-tuple-element.11), channel_id=1, source_target_pairs={{4,0},{8,4},{12,8},{16,12},{20,16},{24,20},{28,24},{5,1},{9,5},{13... | collective-permute-start | bytes 6152 | tf_op jit(solution)/shard_map/ppermute | solution.py:12
  61.8 34.9 %collective-permute-start = (f32[4,128]{1,0:T(4,128)S(1)}, f32[4,128]{1,0:T(4,128)S(1)}, u32[]{:S(2)}, u32[]{:S(2)}) collective-permute-start(f32[4,128]{1,0:T(4,128)S(1)} %get-tuple-element.10), channel_id=1, source_target_pairs={{0,4},{4,8},{8,12},{12,16},{16,20},{20,24},{24,28},{1,5},{5,9},{9,... | collective-permute-start | bytes 6152 | tf_op jit(solution)/shard_map/ppermute | solution.py:12
  69.8 1.1 copy-start.7
  70.1 0.7 copy-start.4
Sparse Core Ops, SparseCore 0:
  70.9 127.4 all-reduce.6
where the time goes:
time: 207 us
  waiting for transfers between devices  71.2 us (34%)
  blocking collectives  63.2 us (31%)
  matrix products  27.7 us (13%)
  between operations  20.2 us (10%)
  local copies, waits for them, and re-layouts  13 us (6%)
  starting transfers between devices  10.4 us (5%)
    psum x1, waiting for transfers between devices, per_device(): kernel_grad = lax.psum(kernel_terms, ('row', 'col'))  71.2 us
    psum x1, blocking collectives, per_device(): col_total = lax.psum(inner_cols, 'row')  24.8 us
    psum x1, blocking collectives, per_device(): row_total = lax.psum(inner_rows, 'col')  15.8 us
    all_gather x1, blocking collectives, per_device(): every_row = lax.all_gather(row_total, 'row', axis=0, tiled=True)  14.2 us
    dot_general x17, matrix products, convolve(): jnp.einsum('ijc,fc->fij', tap_piece, kernel[tap_row + 1, tap_col + 1], pr...  10.5 us
    ppermute x4, starting transfers between devices, shifted(): return lax.ppermute(value, axis, pairs)  10.3 us
    all_gather x1, blocking collectives, per_device(): every_bin = lax.all_gather(embedding, 'col', axis=0, tiled=True)  8.41 us
    dynamic_update_slice x36, local copies, waits for them, and re-layouts, add_into(): lax.dynamic_update_slice_in_dim(target, current + update, position, 0)  8.11 us
  transfers between devices with their start and end apart: 5, of which 1 were waited for; matrix products, arithmetic and copies ran while one was open for 8% of the time, Pallas kernels for 0%

commit v1 on v0

--- a/solution.py
+++ b/solution.py
@@ -4,6 +4,18 @@
 from jax.sharding import PartitionSpec as P
 
 DMAX = 4
+
+
+def doubled_up(x, axis, dim):
+    ways, here, step = (lax.axis_size(axis), lax.axis_index(axis), x.shape[dim])
+    line, have = (x, 1)
+    while have < ways:
+        line = jnp.concatenate(
+            [line, lax.ppermute(line, axis, [(d, (d - have) % ways) for d in range(ways)])],
+            axis=dim,
+        )
+        have = 2 * have
+    return jnp.roll(line, here * step, axis=dim)
 
 
 def shifted(value, axis, by):
@@ -192,7 +204,7 @@
     lower_rows = shifted(row_grad[row_count + margin :], "row", 1)
     inner_rows = fold_edges(row_grad, margin, row_count, lower_rows, upper_rows)
     row_total = lax.psum(inner_rows, "col")
-    every_row = lax.all_gather(row_total, "row", axis=0, tiled=True)
+    every_row = doubled_up(row_total, "row", 0)
     row_share = lax.dynamic_slice_in_dim(every_row, col_start, col_count, 0)
     left_cols = shifted(col_grad[:margin], "col", -1)
     right_cols = shifted(col_grad[col_count + margin :], "col", 1)

time: 207 us -> 207 us (level)
  blocking collectives: 63.2 us -> 50.2 us
  starting transfers between devices: 10.4 us -> 17.2 us
  waiting for transfers between devices: 71.2 us -> 77.3 us
    all_gather x1 -> x0, blocking collectives: 14.2 us -> none  [per_device(): every_row = lax.all_gather(row_total, 'row', axis=0, tiled=True)]
    ppermute x0 -> x3, starting transfers between devices: none -> 6.83 us  [doubled_up(): lax.ppermute(line, axis, [(d, (d - have) % ways) for d in range(ways)])]
    ppermute x0 -> x3, waiting for transfers between devices: none -> 4.1 us  [doubled_up(): lax.ppermute(line, axis, [(d, (d - have) % ways) for d in range(ways)])]
  transfers between devices with their start and end apart: 5 -> 8, of which waited for: 1 -> 3; matrix products, arithmetic and copies ran while one was open for 8% -> 8% of each run, Pallas kernels for 0% -> 0%
where the time goes in v1:
time: 207 us
  waiting for transfers between devices  77.3 us (37%)
  blocking collectives  50.2 us (24%)
  matrix products  27.7 us (13%)
  between operations  20.3 us (10%)
  starting transfers between devices  17.2 us (8%)
  local copies, waits for them, and re-layouts  13 us (6%)
    psum x1, waiting for transfers between devices, per_device(): kernel_grad = lax.psum(kernel_terms, ('row', 'col'))  73.2 us
    psum x1, blocking collectives, per_device(): col_total = lax.psum(inner_cols, 'row')  25.9 us
    psum x1, blocking collectives, per_device(): row_total = lax.psum(inner_rows, 'col')  15.8 us
    dot_general x17, matrix products, convolve(): jnp.einsum('ijc,fc->fij', tap_piece, kernel[tap_row + 1, tap_col + 1], pr...  10.5 us
    ppermute x4, starting transfers between devices, shifted(): return lax.ppermute(value, axis, pairs)  10.3 us
    all_gather x1, blocking collectives, per_device(): every_bin = lax.all_gather(embedding, 'col', axis=0, tiled=True)  8.41 us
    dynamic_update_slice x36, local copies, waits for them, and re-layouts, add_into(): lax.dynamic_update_slice_in_dim(target, current + update, position, 0)  8.11 us
    ppermute x3, starting transfers between devices, doubled_up(): lax.ppermute(line, axis, [(d, (d - have) % ways) for d in range(ways)])  6.83 us
  transfers between devices with their start and end apart: 8, of which 3 were waited for; matrix products, arithmetic and copies ran while one was open for 8% of the time, Pallas kernels for 0%

profile of v1, /device:TPU:8, one launch (start us, length us, event | category | flops | bytes accessed | tf_op | source)
XLA Modules:
  0.0 206.9 jit_solution(4870368362891931498)
XLA Ops:
  7.2 1.3 fusion.300
  13.8 8.4 %all_gather.3 = bf16[256,128]{1,0:T(8,128)(2,1)S(1)} all-gather(bf16[64,128]{1,0:T(8,128)(2,1)} %param.7), channel_id=1, replica_groups=mesh['row'=8,'col'=4] {'col'}, dimensions={0}, use_global_device_ids=true | all-gather | bytes 81920 | tf_op jit(solution)/shard_map/all_gather | solution.py:61
  22.3 0.5 fusion.35
  22.8 0.6 fusion.72
  23.4 0.6 fusion.68
  24.0 0.6 convolution_add_fusion.13
  24.7 0.6 convolution_add_fusion.12
  25.3 0.6 fusion.3
  26.0 0.6 convolution_add_fusion.10
  26.6 0.6 convolution_add_fusion.9
  27.2 0.6 convolution_add_fusion.8
  27.9 0.6 fusion.59
  28.5 0.6 convolution_add_fusion.6
  29.1 0.6 convolution_add_fusion.5
  29.8 0.5 copy-done.3
  30.3 0.6 fusion.1
  30.9 0.6 convolution_add_fusion.3
  31.5 0.6 convolution_add_fusion.2
  32.2 0.6 convolution_add_fusion.1
  32.8 0.6 fusion.2
  33.4 0.6 fusion
  34.1 0.4 bitcast_select_fusion
  44.9 1.3 collective-permute-start.6
  46.2 4.7 %collective-permute-start.5 = (f32[4,128]{1,0:T(4,128)S(1)}, f32[4,128]{1,0:T(4,128)S(1)}, u32[]{:S(2)}, u32[]{:S(2)}) collective-permute-start(f32[4,128]{1,0:T(4,128)S(1)} %get-tuple-element.8), channel_id=1, source_target_pairs={{0,1},{1,2},{2,3},{4,5},{5,6},{6,7},{8,9},{9,10},{10,11},{12,13},{... | collective-permute-start | bytes 6152 | tf_op jit(solution)/shard_map/ppermute | solution.py:24
  50.9 0.5 fusion.272
  51.4 0.5 fusion.270
  51.9 0.5 fusion.264
  52.4 0.5 fusion.268
  52.9 0.5 fusion.266
  56.5 0.5 fusion.262
  59.9 1.9 collective-permute-start.1
  61.8 2.4 %collective-permute-start = (f32[4,128]{1,0:T(4,128)S(1)}, f32[4,128]{1,0:T(4,128)S(1)}, u32[]{:S(2)}, u32[]{:S(2)}) collective-permute-start(f32[4,128]{1,0:T(4,128)S(1)} %get-tuple-element.10), channel_id=1, source_target_pairs={{0,4},{4,8},{8,12},{12,16},{16,20},{20,24},{24,28},{1,5},{5,9},{9,... | collective-permute-start | bytes 6152 | tf_op jit(solution)/shard_map/ppermute | solution.py:24
  67.4 0.3 fusion.13
  67.8 0.3 fusion.16
  68.1 0.3 fusion.19
  68.8 0.3 fusion.25
  69.4 0.3 fusion.31
  70.1 0.7 copy-done.4
  71.2 0.7 copy.11
  71.9 15.8 %psum.21 = f32[32,128]{1,0:T(8,128)S(1)} all-reduce(f32[32,128]{1,0:T(8,128)S(1)} %fusion.95), channel_id=1, replica_groups=mesh['row'=8,'col'=4] {'col'}, use_global_device_ids=true, to_apply=%region_0.1 | all-reduce | flops 4096 | bytes 32768 | tf_op jit(solution)/shard_map/psum | solution.py:206
  87.7 25.9 %psum.22 = f32[64,128]{1,0:T(8,128)S(1)} all-reduce(f32[64,128]{1,0:T(8,128)S(1)} %fusion.93), channel_id=1, replica_groups=mesh['row'=8,'col'=4] {'row'}, use_global_device_ids=true, to_apply=%region_1.2 | all-reduce | flops 8192 | bytes 65536 | tf_op jit(solution)/shard_map/psum | solution.py:212
  113.7 4.2 %collective-permute-start.3 = (f32[64,128]{1,0:T(8,128)S(1)}, f32[64,128]{1,0:T(8,128)S(1)}, u32[]{:S(2)}, u32[]{:S(2)}) collective-permute-start(f32[64,128]{1,0:T(8,128)S(1)} %pad_maximum_fusion.1), channel_id=1, source_target_pairs={{0,24},{4,28},{8,0},{12,4},{16,8},{20,12},{24,16},{28,20},{1,25},{... | collective-permute-start | bytes 98312 | tf_op jit(solution)/shard_map/ppermute | solution.py:14
  117.8 1.6 collective-permute-done.3
  119.4 2.7 %collective-permute-start.4 = (f32[128,128]{1,0:T(8,128)S(1)}, f32[128,128]{1,0:T(8,128)S(1)}, u32[]{:S(2)}, u32[]{:S(2)}) collective-permute-start(f32[128,128]{1,0:T(8,128)S(1)} %pad_maximum_fusion), channel_id=1, source_target_pairs={{0,16},{4,20},{8,24},{12,28},{16,0},{20,4},{24,8},{28,12},{1,17},{... | collective-permute-start | bytes 196616 | tf_op jit(solution)/shard_map/ppermute | solution.py:14
  122.1 2.5 %collective-permute-done.4 = f32[128,128]{1,0:T(8,128)S(1)} collective-permute-done((f32[128,128]{1,0:T(8,128)S(1)}, f32[128,128]{1,0:T(8,128)S(1)}, u32[]{:S(2)}, u32[]{:S(2)}) %collective-permute-start.4) | collective-permute-done | bytes 65568 | tf_op jit(solution)/shard_map/ppermute | solution.py:14
  124.7 0.6 add_multiply_fusion
  125.3 73.2 %all-reduce.7.cloned.1.call-done = f32[3,3,48,128]{3,2,1,0:T(8,128)} async-done(((f32[3,3,48,128]{3,2,1,0:T(8,128)}), f32[3,3,48,128]{3,2,1,0:T(8,128)}) %all-reduce.7.cloned.1.call-update) | async-done | bytes 221200 | tf_op jit(solution)/shard_map/psum | solution.py:131
  198.5 1.6 copy.94
  (138 shorter events, 20.6 us)
Async XLA Ops:
  7.2 26.9 %copy-start = (bf16[5,32,64]{2,1,0:T(8,128)(2,1)S(1)}, bf16[5,32,64]{2,1,0:T(8,128)(2,1)}, u32[]{:S(2)}) copy-start(bf16[5,32,64]{2,1,0:T(8,128)(2,1)} %param.13) | copy-start | bytes 61444
  7.2 15.6 %copy-start.1 = (bf16[3,3,48,128]{3,2,1,0:T(8,128)(2,1)S(1)}, bf16[3,3,48,128]{3,2,1,0:T(8,128)(2,1)}, u32[]{:S(2)}) copy-start(bf16[3,3,48,128]{3,2,1,0:T(8,128)(2,1)} %param.9) | copy-start | bytes 331780
  7.2 191.3 %all-reduce.7.cloned.1.call-start = ((), (), s32[]{:S(2)}) async-start(), calls=%async_computation | async-start | bytes 442368 | tf_op jit(solution)/shard_map/psum | solution.py:131
  23.4 1.9 copy-start.2
  29.1 1.1 copy-start.3
  32.1 0.7 copy-start.6
  33.4 0.7 copy-start.5
  44.9 42.8 %collective-permute-start.6 = (f32[4,128]{1,0:T(4,128)S(1)}, f32[4,128]{1,0:T(4,128)S(1)}, u32[]{:S(2)}, u32[]{:S(2)}) collective-permute-start(f32[4,128]{1,0:T(4,128)S(1)} %get-tuple-element.9), channel_id=1, source_target_pairs={{1,0},{2,1},{3,2},{5,4},{6,5},{7,6},{9,8},{10,9},{11,10},{13,12},{... | collective-permute-start | bytes 6152 | tf_op jit(solution)/shard_map/ppermute | solution.py:24
  46.2 41.5 %collective-permute-start.5 = (f32[4,128]{1,0:T(4,128)S(1)}, f32[4,128]{1,0:T(4,128)S(1)}, u32[]{:S(2)}, u32[]{:S(2)}) collective-permute-start(f32[4,128]{1,0:T(4,128)S(1)} %get-tuple-element.8), channel_id=1, source_target_pairs={{0,1},{1,2},{2,3},{4,5},{5,6},{6,7},{8,9},{9,10},{10,11},{12,13},{... | collective-permute-start | bytes 6152 | tf_op jit(solution)/shard_map/ppermute | solution.py:24
  59.9 12.0 %collective-permute-start.1 = (f32[4,128]{1,0:T(4,128)S(1)}, f32[4,128]{1,0:T(4,128)S(1)}, u32[]{:S(2)}, u32[]{:S(2)}) collective-permute-start(f32[4,128]{1,0:T(4,128)S(1)} %get-tuple-element.11), channel_id=1, source_target_pairs={{4,0},{8,4},{12,8},{16,12},{20,16},{24,20},{28,24},{5,1},{9,5},{13... | collective-permute-start | bytes 6152 | tf_op jit(solution)/shard_map/ppermute | solution.py:24
  61.8 10.1 %collective-permute-start = (f32[4,128]{1,0:T(4,128)S(1)}, f32[4,128]{1,0:T(4,128)S(1)}, u32[]{:S(2)}, u32[]{:S(2)}) collective-permute-start(f32[4,128]{1,0:T(4,128)S(1)} %get-tuple-element.10), channel_id=1, source_target_pairs={{0,4},{4,8},{8,12},{12,16},{16,20},{20,24},{24,28},{1,5},{5,9},{9,... | collective-permute-start | bytes 6152 | tf_op jit(solution)/shard_map/ppermute | solution.py:24
  69.8 1.1 copy-start.7
  70.1 0.7 copy-start.4
  87.7 26.0 %collective-permute-start.2 = (f32[32,128]{1,0:T(8,128)S(1)}, f32[32,128]{1,0:T(8,128)S(1)}, u32[]{:S(2)}, u32[]{:S(2)}) collective-permute-start(f32[32,128]{1,0:T(8,128)S(1)} %psum.21), channel_id=1, source_target_pairs={{0,28},{4,0},{8,4},{12,8},{16,12},{20,16},{24,20},{28,24},{1,29},{... | collective-permute-start | bytes 49160 | tf_op jit(solution)/shard_map/ppermute | solution.py:14
  113.7 5.8 %collective-permute-start.3 = (f32[64,128]{1,0:T(8,128)S(1)}, f32[64,128]{1,0:T(8,128)S(1)}, u32[]{:S(2)}, u32[]{:S(2)}) collective-permute-start(f32[64,128]{1,0:T(8,128)S(1)} %pad_maximum_fusion.1), channel_id=1, source_target_pairs={{0,24},{4,28},{8,0},{12,4},{16,8},{20,12},{24,16},{28,20},{1,25},{... | collective-permute-start | bytes 98312 | tf_op jit(solution)/shard_map/ppermute | solution.py:14
  119.4 5.2 %collective-permute-start.4 = (f32[128,128]{1,0:T(8,128)S(1)}, f32[128,128]{1,0:T(8,128)S(1)}, u32[]{:S(2)}, u32[]{:S(2)}) collective-permute-start(f32[128,128]{1,0:T(8,128)S(1)} %pad_maximum_fusion), channel_id=1, source_target_pairs={{0,16},{4,20},{8,24},{12,28},{16,0},{20,4},{24,8},{28,12},{1,17},{... | collective-permute-start | bytes 196616 | tf_op jit(solution)/shard_map/ppermute | solution.py:14
Sparse Core Ops, SparseCore 0:
  70.9 127.4 all-reduce.6
